TPU v7x, 32 devices: a whole 2x2x4 slice. The times are simulated.
32 devices in a mesh: dp: 2 (over x), hp: 4 (over z), cp: 4 (over y, core).
Axes of the slice: x: 2, y: 2, z: 4, core: 2. Of those that a mesh axis runs over, the one named last changes fastest.
Arguments:
- latent: bfloat16 [256, 16, 96, 128], P(('dp', 'cp'), 'hp'), parts along dimension 0
- conv_w: bfloat16 [4, 3, 3, 3, 128, 128], replicated
- conv_b: float32 [4, 128], replicated
- gn_gamma: float32 [4, 128], replicated
- gn_beta: float32 [4, 128], replicated
Outputs:
- output: bfloat16 [256, 16, 96, 128], P(('dp', 'cp'), 'hp'), parts along dimension 0
There are 2 independent parts. A program takes and returns all parts, laid end to end along the dimension named above; an argument that names none is the same for every part.
All inputs are finite; a program needn't handle non-finite values.
Results may differ from a plain program's by a relative error of at most 0.00957576.
Values are sent between devices in bfloat16 or wider.
A program may use at most 1 GiB of HBM per device.

v0:
```python
import jax
import jax.numpy as jnp
from jax import lax
from jax.sharding import PartitionSpec as P

GROUPS = 32
EPS = 1e-6


def norm_silu(local_act, gamma, beta, total_count):
    frames, row_count, lat_width, channels = local_act.shape
    per_group = channels // GROUPS
    grouped = local_act.reshape(frames, row_count, lat_width, GROUPS, per_group).astype(jnp.float32)
    stat_sums = jnp.stack([jnp.sum(grouped, axis=(0, 1, 2, 4)), jnp.sum(grouped * grouped, axis=(0, 1, 2, 4))])
    stat_sums = lax.psum(stat_sums, ("cp", "hp"))
    mean_val = stat_sums[0] / total_count
    variance = stat_sums[1] / total_count - mean_val * mean_val
    inv_std = lax.rsqrt(variance + EPS)
    gamma_g = gamma.reshape(GROUPS, per_group)
    scale_c = (inv_std[:, None] * gamma_g).reshape(channels)
    shift_c = (beta.reshape(GROUPS, per_group) - (mean_val * inv_std)[:, None] * gamma_g).reshape(channels)
    return jax.nn.silu(local_act.astype(jnp.float32) * scale_c + shift_c).astype(jnp.bfloat16)


def conv_valid(padded, kernel, bias_vec):
    conv_out = lax.conv_general_dilated(padded[None], kernel, (1, 1, 1), ((0, 0), (0, 0), (1, 1)), dimension_numbers=("NDHWC", "DHWIO", "NDHWC"), preferred_element_type=jnp.float32)
    return (conv_out[0] + bias_vec).astype(jnp.bfloat16)


def solution(mesh):
    n_time = mesh.shape["cp"]
    n_rows = mesh.shape["hp"]
    time_fwd = [(i, i + 1) for i in range(n_time - 1)]
    rows_down = [(i, i + 1) for i in range(n_rows - 1)]
    rows_up = [(i + 1, i) for i in range(n_rows - 1)]

    def local_decode(local_lat, conv_w, conv_b, gn_gamma, gn_beta):
        frames, row_count, lat_width, channels = local_lat.shape
        total_count = frames * n_time * row_count * n_rows * lat_width * (channels // GROUPS)
        time_rank = lax.axis_index("cp")
        residual = local_lat
        for block_idx in range(2):
            hidden = residual
            for sub_idx in range(2):
                layer_idx = 2 * block_idx + sub_idx
                activated = norm_silu(hidden, gn_gamma[layer_idx], gn_beta[layer_idx], total_count)
                prev_frames = lax.ppermute(activated[frames - 2:], "cp", time_fwd)
                own_first = jnp.broadcast_to(activated[:1], prev_frames.shape)
                prev_frames = jnp.where(time_rank == 0, own_first, prev_frames)
                extended = jnp.concatenate([prev_frames, activated], axis=0)
                from_above = lax.ppermute(extended[:, row_count - 1:], "hp", rows_down)
                from_below = lax.ppermute(extended[:, :1], "hp", rows_up)
                extended = jnp.concatenate([from_above, extended, from_below], axis=1)
                hidden = conv_valid(extended, conv_w[layer_idx], conv_b[layer_idx])
            residual = (residual.astype(jnp.float32) + hidden.astype(jnp.float32)).astype(jnp.bfloat16)
        return residual

    video_spec = P(("dp", "cp"), "hp", None, None)
    return jax.shard_map(local_decode, mesh=mesh, in_specs=(video_spec, P(), P(), P(), P()), out_specs=video_spec, check_vma=False)
```

profile of v0, /device:TPU:4, one launch (start us, length us, event | category | flops | bytes accessed | tf_op | source)
XLA Modules:
  0.0 505.9 jit_solution(3979975688891688596)
XLA Ops:
  0.0 3.5 convert_reduce_fusion.1
  4.0 32.7 %psum.28 = f32[2,32]{1,0:T(2,128)S(1)} all-reduce(f32[2,32]{1,0:T(2,128)S(1)} %pad_maximum_fusion.8), channel_id=1, replica_groups=mesh['dp'=2,'hp'=4,'cp'=4] {'cp','hp'}, use_global_device_ids=true, to_apply=%region_4.5 | all-reduce | flops 64 | bytes 512 | tf_op jit(solution)/shard_map/psum | solution.py:15
  37.8 3.3 fusion.17
  41.1 1.9 collective-permute-start
  43.0 5.0 collective-permute-done
  51.4 12.7 %collective-permute-done.1 = bf16[34,1,96,128]{3,2,1,0:T(8,128)(2,1)S(1)} collective-permute-done((bf16[34,1,96,128]{3,2,1,0:T(8,128)(2,1)S(1)}, bf16[34,1,96,128]{3,2,1,0:T(8,128)(2,1)S(1)}, u32[]{:S(2)}, u32[]{:S(2)}) %collective-permute-start.1) | collective-permute-done | bytes 835616 | tf_op jit(solution)/shard_map/ppermute | solution.py:51
  64.2 4.2 collective-permute-done.2
  69.1 5.5 %pad = bf16[34,6,1,104,128]{4,3,1,0,2:T(8,128)(2,1)} pad(bf16[34,6,1,96,128]{4,3,1,0,2:T(8,128)(2,1)S(1)} %maximum_bitcast_fusion, bf16[]{:T(256)} %constant.26), padding=0_0x0_0x0_0x1_7x0_0 | pad | bytes 10444802 | tf_op jit(solution)/shard_map/broadcast_in_dim | solution.py:26
  74.6 9.7 %reshape.240 = bf16[34,6,1,8,13,128]{5,4,3,1,0,2:T(8,128)(2,1)} reshape(bf16[34,6,1,104,128]{4,3,1,0,2:T(8,128)(2,1)} %pad) | data formatting | bytes 10862592 | tf_op jit(solution)/shard_map/conv_general_dilated | solution.py:26
  84.3 5.7 %copy.25 = bf16[34,6,1,8,13,128]{5,3,4,1,0,2:T(8,128)(2,1)S(1)} copy(bf16[34,6,1,8,13,128]{5,4,3,1,0,2:T(8,128)(2,1)} %reshape.240) | data formatting | bytes 10862592 | tf_op jit(solution)/shard_map/conv_general_dilated | solution.py:26
  90.2 28.9 %fusion.4 = (f32[128]{0:T(128)S(1)}, f32[128]{0:T(128)S(1)}, f32[32,4,8,13,128]{4,2,3,1,0:T(8,128)}) fusion(pred[8,13]{0,1:T(8,128)(4,1)S(1)} %copy-done.5, f32[128]{0:T(128)S(1)} %get-tuple-element.32, bf16[4,3,3,3,128,128]{5,4,3,2,1,0:T(8,128)(2,1)} %param.6, bf16[34,6,1,7,2,128]{5,3,4,1,0,2:T(8,128)(2,1)S(1)} %slice.170, ...), kind=kOutput, calls=%fused_computation.17 | convolution fusion | flops 11811741696 | bytes 13864552 | tf_op jit(solution)/shard_map/conv_general_dilated | solution.py:26
  119.6 30.3 %psum.29 = f32[2,32]{1,0:T(2,128)S(1)} all-reduce(f32[2,32]{1,0:T(2,128)S(1)} %pad_maximum_fusion.9), channel_id=1, replica_groups=mesh['dp'=2,'hp'=4,'cp'=4] {'cp','hp'}, use_global_device_ids=true, to_apply=%region_9.10 | all-reduce | flops 64 | bytes 512 | tf_op jit(solution)/shard_map/psum | solution.py:15
  150.3 6.9 %copy.26 = f32[32,4,8,13,128]{4,0,3,2,1:T(8,128)S(1)} copy(f32[32,4,8,13,128]{4,2,3,1,0:T(8,128)} %get-tuple-element.42) | data formatting | bytes 13631488 | tf_op jit(solution)/shard_map/conv_general_dilated | solution.py:26
  158.0 6.7 %multiply_convert_fusion.1 = bf16[32,4,96,128]{3,2,1,0:T(8,128)(2,1)S(1)} fusion(f32[32,4,1,96,128]{4,0,3,1,2:T(8,128)S(1)} %slice.171, f32[128]{0:T(128)S(1)} %get-tuple-element.39, f32[128]{0:T(128)S(1)} %get-tuple-element.38, f32[128]{0:T(128)S(1)} %get-tuple-element.32), kind=kLoop, calls=%fused_computation.56 | loop fusion | flops 15728640 | bytes 9438720 | tf_op jit(solution)/shard_map/convert_element_type | solution.py:22
  164.7 1.9 collective-permute-start.3
  166.7 5.0 collective-permute-done.3
  171.9 3.8 collective-permute-start.4
  177.0 13.0 %collective-permute-done.4 = bf16[34,1,96,128]{3,2,1,0:T(8,128)(2,1)S(1)} collective-permute-done((bf16[34,1,96,128]{3,2,1,0:T(8,128)(2,1)S(1)}, bf16[34,1,96,128]{3,2,1,0:T(8,128)(2,1)S(1)}, u32[]{:S(2)}, u32[]{:S(2)}) %collective-permute-start.4) | collective-permute-done | bytes 835616 | tf_op jit(solution)/shard_map/ppermute | solution.py:51
  190.0 4.2 collective-permute-done.5
  195.4 5.5 %pad.2 = bf16[34,6,1,104,128]{4,3,1,0,2:T(8,128)(2,1)} pad(bf16[34,6,1,96,128]{4,3,1,0,2:T(8,128)(2,1)S(1)} %maximum_bitcast_fusion.1, bf16[]{:T(256)} %constant.26), padding=0_0x0_0x0_0x1_7x0_0 | pad | bytes 10444802 | tf_op jit(solution)/shard_map/broadcast_in_dim | solution.py:26
  200.9 9.7 %reshape.249 = bf16[34,6,1,8,13,128]{5,4,3,1,0,2:T(8,128)(2,1)} reshape(bf16[34,6,1,104,128]{4,3,1,0,2:T(8,128)(2,1)} %pad.2) | data formatting | bytes 10862592 | tf_op jit(solution)/shard_map/conv_general_dilated | solution.py:26
  210.5 5.7 %copy.29 = bf16[34,6,1,8,13,128]{5,3,4,1,0,2:T(8,128)(2,1)S(1)} copy(bf16[34,6,1,8,13,128]{5,4,3,1,0,2:T(8,128)(2,1)} %reshape.249) | data formatting | bytes 10862592 | tf_op jit(solution)/shard_map/conv_general_dilated | solution.py:26
  216.4 27.5 %broadcast_select_fusion.2 = f32[32,4,8,13,128]{4,2,3,1,0:T(8,128)S(1)} fusion(pred[8,13]{0,1:T(8,128)(4,1)S(1)} %copy-done.5, bf16[34,6,1,7,2,128]{5,3,4,1,0,2:T(8,128)(2,1)S(1)} %slice.174, bf16[34,6,1,8,13,128]{5,3,4,1,0,2:T(8,128)(2,1)S(1)} %copy.29, bf16[4,3,3,3,128,128]{5,4,3,2,1,0:T(8,128)(2,1)} %param.6), kind=kOutput, calls=%fused_computation.87 | convolution fusion | flops 11798110208 | bytes 13863016 | tf_op jit(solution)/shard_map/conv_general_dilated | solution.py:26
  243.9 3.9 copy.30
  249.7 6.9 %convert_reduce_fusion = (f32[128]{0:T(128)S(1)}, f32[128]{0:T(128)S(1)}, bf16[32,4,96,128]{3,2,1,0:T(8,128)(2,1)S(1)}) fusion(f32[128]{0:T(128)S(1)} %get-tuple-element.31, f32[32,4,1,96,128]{4,0,3,1,2:T(8,128)S(1)} %slice.175, bf16[32,4,96,128]{3,2,1,0:T(8,128)(2,1)S(1)} %copy-done), kind=kLoop, calls=%fused_computation.8 | loop fusion | flops 15728384 | bytes 12584448 | tf_op jit(solution)/shard_map/reduce_sum | solution.py:14
  257.2 29.9 %psum.30 = f32[2,32]{1,0:T(2,128)S(1)} all-reduce(f32[2,32]{1,0:T(2,128)S(1)} %pad_maximum_fusion.10), channel_id=1, replica_groups=mesh['dp'=2,'hp'=4,'cp'=4] {'cp','hp'}, use_global_device_ids=true, to_apply=%region_14.15 | all-reduce | flops 64 | bytes 512 | tf_op jit(solution)/shard_map/psum | solution.py:15
  289.4 1.9 collective-permute-start.6
  291.3 5.0 collective-permute-done.6
  296.6 4.0 collective-permute-start.7
  301.9 13.0 %collective-permute-done.7 = bf16[34,1,96,128]{3,2,1,0:T(8,128)(2,1)S(1)} collective-permute-done((bf16[34,1,96,128]{3,2,1,0:T(8,128)(2,1)S(1)}, bf16[34,1,96,128]{3,2,1,0:T(8,128)(2,1)S(1)}, u32[]{:S(2)}, u32[]{:S(2)}) %collective-permute-start.7) | collective-permute-done | bytes 835616 | tf_op jit(solution)/shard_map/ppermute | solution.py:51
  314.9 4.2 collective-permute-done.8
  320.1 5.5 %pad.4 = bf16[34,6,1,104,128]{4,3,1,0,2:T(8,128)(2,1)} pad(bf16[34,6,1,96,128]{4,3,1,0,2:T(8,128)(2,1)S(1)} %maximum_bitcast_fusion.2, bf16[]{:T(256)} %constant.26), padding=0_0x0_0x0_0x1_7x0_0 | pad | bytes 10444802 | tf_op jit(solution)/shard_map/broadcast_in_dim | solution.py:26
  325.6 9.7 %reshape.256 = bf16[34,6,1,8,13,128]{5,4,3,1,0,2:T(8,128)(2,1)} reshape(bf16[34,6,1,104,128]{4,3,1,0,2:T(8,128)(2,1)} %pad.4) | data formatting | bytes 10862592 | tf_op jit(solution)/shard_map/conv_general_dilated | solution.py:26
  335.2 5.7 %copy.33 = bf16[34,6,1,8,13,128]{5,3,4,1,0,2:T(8,128)(2,1)S(1)} copy(bf16[34,6,1,8,13,128]{5,4,3,1,0,2:T(8,128)(2,1)} %reshape.256) | data formatting | bytes 10862592 | tf_op jit(solution)/shard_map/conv_general_dilated | solution.py:26
  341.1 29.2 %fusion.7 = (f32[128]{0:T(128)S(1)}, f32[128]{0:T(128)S(1)}, f32[32,4,8,13,128]{4,2,3,1,0:T(8,128)}) fusion(pred[8,13]{0,1:T(8,128)(4,1)S(1)} %copy-done.5, f32[128]{0:T(128)S(1)} %get-tuple-element.33, bf16[4,3,3,3,128,128]{5,4,3,2,1,0:T(8,128)(2,1)} %param.6, bf16[34,6,1,7,2,128]{5,3,4,1,0,2:T(8,128)(2,1)S(1)} %slice.178, ...), kind=kOutput, calls=%fused_computation.20 | convolution fusion | flops 11811741696 | bytes 13864552 | tf_op jit(solution)/shard_map/conv_general_dilated | solution.py:26
  370.8 30.1 %psum.31 = f32[2,32]{1,0:T(2,128)S(1)} all-reduce(f32[2,32]{1,0:T(2,128)S(1)} %pad_maximum_fusion.11), channel_id=1, replica_groups=mesh['dp'=2,'hp'=4,'cp'=4] {'cp','hp'}, use_global_device_ids=true, to_apply=%region_19.20 | all-reduce | flops 64 | bytes 512 | tf_op jit(solution)/shard_map/psum | solution.py:15
  401.2 6.9 %copy.34 = f32[32,4,8,13,128]{4,0,3,2,1:T(8,128)S(1)} copy(f32[32,4,8,13,128]{4,2,3,1,0:T(8,128)} %get-tuple-element.43) | data formatting | bytes 13631488 | tf_op jit(solution)/shard_map/conv_general_dilated | solution.py:26
  408.8 6.7 %multiply_convert_fusion = bf16[32,4,96,128]{3,2,1,0:T(8,128)(2,1)S(1)} fusion(f32[32,4,1,96,128]{4,0,3,1,2:T(8,128)S(1)} %slice.179, f32[128]{0:T(128)S(1)} %get-tuple-element.35, f32[128]{0:T(128)S(1)} %get-tuple-element.34, f32[128]{0:T(128)S(1)} %get-tuple-element.33), kind=kLoop, calls=%fused_computation.55 | loop fusion | flops 15728640 | bytes 9438720 | tf_op jit(solution)/shard_map/convert_element_type | solution.py:22
  417.5 5.0 collective-permute-done.9
  422.7 4.0 collective-permute-start.10
  428.0 13.0 %collective-permute-done.10 = bf16[34,1,96,128]{3,2,1,0:T(8,128)(2,1)S(1)} collective-permute-done((bf16[34,1,96,128]{3,2,1,0:T(8,128)(2,1)S(1)}, bf16[34,1,96,128]{3,2,1,0:T(8,128)(2,1)S(1)}, u32[]{:S(2)}, u32[]{:S(2)}) %collective-permute-start.10) | collective-permute-done | bytes 835616 | tf_op jit(solution)/shard_map/ppermute | solution.py:51
  441.0 4.2 collective-permute-done.11
  446.2 5.5 %pad.6 = bf16[34,6,1,104,128]{4,3,1,0,2:T(8,128)(2,1)} pad(bf16[34,6,1,96,128]{4,3,1,0,2:T(8,128)(2,1)S(1)} %maximum_bitcast_fusion.3, bf16[]{:T(256)} %constant.26), padding=0_0x0_0x0_0x1_7x0_0 | pad | bytes 10444802 | tf_op jit(solution)/shard_map/broadcast_in_dim | solution.py:26
  451.7 9.7 %reshape.265 = bf16[34,6,1,8,13,128]{5,4,3,1,0,2:T(8,128)(2,1)} reshape(bf16[34,6,1,104,128]{4,3,1,0,2:T(8,128)(2,1)} %pad.6) | data formatting | bytes 10862592 | tf_op jit(solution)/shard_map/conv_general_dilated | solution.py:26
  461.4 5.7 %copy.37 = bf16[34,6,1,8,13,128]{5,3,4,1,0,2:T(8,128)(2,1)S(1)} copy(bf16[34,6,1,8,13,128]{5,4,3,1,0,2:T(8,128)(2,1)} %reshape.265) | data formatting | bytes 10862592 | tf_op jit(solution)/shard_map/conv_general_dilated | solution.py:26
  467.2 27.8 %broadcast_select_fusion = f32[32,4,8,13,128]{4,2,3,1,0:T(8,128)S(1)} fusion(pred[8,13]{0,1:T(8,128)(4,1)S(1)} %copy-done.5, bf16[34,6,1,7,2,128]{5,3,4,1,0,2:T(8,128)(2,1)S(1)} %slice.182, bf16[34,6,1,8,13,128]{5,3,4,1,0,2:T(8,128)(2,1)S(1)} %copy.37, bf16[4,3,3,3,128,128]{5,4,3,2,1,0:T(8,128)(2,1)} %param.6), kind=kOutput, calls=%fused_computation.85 | convolution fusion | flops 11798110208 | bytes 13863016 | tf_op jit(solution)/shard_map/conv_general_dilated | solution.py:26
  495.1 3.9 copy.38
  499.8 5.7 %fusion.27 = bf16[32,4,96,128]{3,2,1,0:T(8,128)(2,1)} fusion(bf16[32,4,96,128]{3,2,1,0:T(8,128)(2,1)S(1)} %get-tuple-element.17, f32[32,4,1,96,128]{4,0,3,1,2:T(8,128)S(1)} %slice.183, f32[128]{0:T(128)S(1)} %copy-done.1), kind=kLoop, calls=%fused_computation.42 | loop fusion | flops 9437184 | bytes 12583424 | tf_op jit(solution)/shard_map/convert_element_type | solution.py:55
  (92 shorter events, 24.4 us)
Async XLA Ops:
  3.5 47.4 %copy-start.2 = (f32[4,128]{1,0:T(4,128)S(1)}, f32[4,128]{1,0:T(4,128)}, u32[]{:S(2)}) copy-start(f32[4,128]{1,0:T(4,128)} %param.7) | copy-start | bytes 6148
  41.1 7.0 %collective-permute-start = (bf16[2,4,96,128]{3,2,1,0:T(8,128)(2,1)S(1)}, bf16[2,4,96,128]{3,2,1,0:T(8,128)(2,1)S(1)}, u32[]{:S(2)}, u32[]{:S(2)}) collective-permute-start(bf16[2,4,96,128]{3,2,1,0:T(8,128)(2,1)S(1)} %slice.169), channel_id=1, source_target_pairs={{0,1},{1,2},{2,3},{4,5},{5,6},{6,7},{8,9},{9,10},{10,11},{12,13},{... | collective-permute-start | bytes 589832 | tf_op jit(solution)/shard_map/ppermute | solution.py:47
  48.2 15.9 %collective-permute-start.1 = (bf16[34,1,96,128]{3,2,1,0:T(8,128)(2,1)S(1)}, bf16[34,1,96,128]{3,2,1,0:T(8,128)(2,1)S(1)}, u32[]{:S(2)}, u32[]{:S(2)}) collective-permute-start(bf16[34,1,96,128]{3,2,1,0:T(8,128)(2,1)S(1)} %get-tuple-element.28), channel_id=1, source_target_pairs={{0,4},{4,8},{8,12},{1,5},{5,9},{9,13},{2,6},{6,10},{10,14},{3,7},{... | collective-permute-start | bytes 2506760 | tf_op jit(solution)/shard_map/ppermute | solution.py:51
  49.6 18.8 %collective-permute-start.2 = (bf16[34,1,96,128]{3,2,1,0:T(8,128)(2,1)S(1)}, bf16[34,1,96,128]{3,2,1,0:T(8,128)(2,1)S(1)}, u32[]{:S(2)}, u32[]{:S(2)}) collective-permute-start(bf16[34,1,96,128]{3,2,1,0:T(8,128)(2,1)S(1)} %get-tuple-element.29), channel_id=1, source_target_pairs={{4,0},{8,4},{12,8},{5,1},{9,5},{13,9},{6,2},{10,6},{14,10},{7,3},{... | collective-permute-start | bytes 2506760 | tf_op jit(solution)/shard_map/ppermute | solution.py:52
  84.3 5.9 %copy-start.5 = (pred[8,13]{0,1:T(8,128)(4,1)S(1)}, pred[8,13]{0,1:T(8,128)(4,1)}, u32[]{:S(2)}) copy-start(pred[8,13]{0,1:T(8,128)(4,1)} %constant.46) | copy-start | bytes 316
  157.2 0.7 copy-start.3
  157.2 0.7 copy-start.4
  164.7 7.0 %collective-permute-start.3 = (bf16[2,4,96,128]{3,2,1,0:T(8,128)(2,1)S(1)}, bf16[2,4,96,128]{3,2,1,0:T(8,128)(2,1)S(1)}, u32[]{:S(2)}, u32[]{:S(2)}) collective-permute-start(bf16[2,4,96,128]{3,2,1,0:T(8,128)(2,1)S(1)} %slice.173), channel_id=1, source_target_pairs={{0,1},{1,2},{2,3},{4,5},{5,6},{6,7},{8,9},{9,10},{10,11},{12,13},{... | collective-permute-start | bytes 589832 | tf_op jit(solution)/shard_map/ppermute | solution.py:47
  171.9 18.1 %collective-permute-start.4 = (bf16[34,1,96,128]{3,2,1,0:T(8,128)(2,1)S(1)}, bf16[34,1,96,128]{3,2,1,0:T(8,128)(2,1)S(1)}, u32[]{:S(2)}, u32[]{:S(2)}) collective-permute-start(bf16[34,1,96,128]{3,2,1,0:T(8,128)(2,1)S(1)} %get-tuple-element.26), channel_id=1, source_target_pairs={{0,4},{4,8},{8,12},{1,5},{5,9},{9,13},{2,6},{6,10},{10,14},{3,7},{... | collective-permute-start | bytes 2506760 | tf_op jit(solution)/shard_map/ppermute | solution.py:51
  175.7 18.5 %collective-permute-start.5 = (bf16[34,1,96,128]{3,2,1,0:T(8,128)(2,1)S(1)}, bf16[34,1,96,128]{3,2,1,0:T(8,128)(2,1)S(1)}, u32[]{:S(2)}, u32[]{:S(2)}) collective-permute-start(bf16[34,1,96,128]{3,2,1,0:T(8,128)(2,1)S(1)} %get-tuple-element.27), channel_id=1, source_target_pairs={{4,0},{8,4},{12,8},{5,1},{9,5},{13,9},{6,2},{10,6},{14,10},{7,3},{... | collective-permute-start | bytes 2506760 | tf_op jit(solution)/shard_map/ppermute | solution.py:52
  247.8 1.9 copy-start
  289.4 7.0 %collective-permute-start.6 = (bf16[2,4,96,128]{3,2,1,0:T(8,128)(2,1)S(1)}, bf16[2,4,96,128]{3,2,1,0:T(8,128)(2,1)S(1)}, u32[]{:S(2)}, u32[]{:S(2)}) collective-permute-start(bf16[2,4,96,128]{3,2,1,0:T(8,128)(2,1)S(1)} %slice.177), channel_id=1, source_target_pairs={{0,1},{1,2},{2,3},{4,5},{5,6},{6,7},{8,9},{9,10},{10,11},{12,13},{... | collective-permute-start | bytes 589832 | tf_op jit(solution)/shard_map/ppermute | solution.py:47
  296.6 18.3 %collective-permute-start.7 = (bf16[34,1,96,128]{3,2,1,0:T(8,128)(2,1)S(1)}, bf16[34,1,96,128]{3,2,1,0:T(8,128)(2,1)S(1)}, u32[]{:S(2)}, u32[]{:S(2)}) collective-permute-start(bf16[34,1,96,128]{3,2,1,0:T(8,128)(2,1)S(1)} %get-tuple-element.24), channel_id=1, source_target_pairs={{0,4},{4,8},{8,12},{1,5},{5,9},{9,13},{2,6},{6,10},{10,14},{3,7},{... | collective-permute-start | bytes 2506760 | tf_op jit(solution)/shard_map/ppermute | solution.py:51
  300.6 18.5 %collective-permute-start.8 = (bf16[34,1,96,128]{3,2,1,0:T(8,128)(2,1)S(1)}, bf16[34,1,96,128]{3,2,1,0:T(8,128)(2,1)S(1)}, u32[]{:S(2)}, u32[]{:S(2)}) collective-permute-start(bf16[34,1,96,128]{3,2,1,0:T(8,128)(2,1)S(1)} %get-tuple-element.25), channel_id=1, source_target_pairs={{4,0},{8,4},{12,8},{5,1},{9,5},{13,9},{6,2},{10,6},{14,10},{7,3},{... | collective-permute-start | bytes 2506760 | tf_op jit(solution)/shard_map/ppermute | solution.py:52
  415.6 7.0 %collective-permute-start.9 = (bf16[2,4,96,128]{3,2,1,0:T(8,128)(2,1)S(1)}, bf16[2,4,96,128]{3,2,1,0:T(8,128)(2,1)S(1)}, u32[]{:S(2)}, u32[]{:S(2)}) collective-permute-start(bf16[2,4,96,128]{3,2,1,0:T(8,128)(2,1)S(1)} %slice.181), channel_id=1, source_target_pairs={{0,1},{1,2},{2,3},{4,5},{5,6},{6,7},{8,9},{9,10},{10,11},{12,13},{... | collective-permute-start | bytes 589832 | tf_op jit(solution)/shard_map/ppermute | solution.py:47
  422.7 18.3 %collective-permute-start.10 = (bf16[34,1,96,128]{3,2,1,0:T(8,128)(2,1)S(1)}, bf16[34,1,96,128]{3,2,1,0:T(8,128)(2,1)S(1)}, u32[]{:S(2)}, u32[]{:S(2)}) collective-permute-start(bf16[34,1,96,128]{3,2,1,0:T(8,128)(2,1)S(1)} %get-tuple-element.22), channel_id=1, source_target_pairs={{0,4},{4,8},{8,12},{1,5},{5,9},{9,13},{2,6},{6,10},{10,14},{3,7},{... | collective-permute-start | bytes 2506760 | tf_op jit(solution)/shard_map/ppermute | solution.py:51
  426.7 18.5 %collective-permute-start.11 = (bf16[34,1,96,128]{3,2,1,0:T(8,128)(2,1)S(1)}, bf16[34,1,96,128]{3,2,1,0:T(8,128)(2,1)S(1)}, u32[]{:S(2)}, u32[]{:S(2)}) collective-permute-start(bf16[34,1,96,128]{3,2,1,0:T(8,128)(2,1)S(1)} %get-tuple-element.23), channel_id=1, source_target_pairs={{4,0},{8,4},{12,8},{5,1},{9,5},{13,9},{6,2},{10,6},{14,10},{7,3},{... | collective-permute-start | bytes 2506760 | tf_op jit(solution)/shard_map/ppermute | solution.py:52
  499.0 0.7 copy-start.1
where the time goes:
time: 515 us; the launch traced here: 506 us
  blocking collectives  123 us (24%)
  local copies, waits for them, and re-layouts  113 us (22%)
  matrix products  113 us (22%)
  waiting for transfers between devices  88.6 us (17%)
  other arithmetic  41.1 us (8%)
  starting transfers between devices  26 us (5%)
    psum x4, blocking collectives, norm_silu(): stat_sums = lax.psum(stat_sums, ('cp', 'hp'))  123 us
    conv_general_dilated x4, matrix products, conv_valid(): lax.conv_general_dilated(padded[None], kernel, (1, 1, 1), ((0, 0), (0, 0)...  113 us
    conv_general_dilated x20, local copies, waits for them, and re-layouts, conv_valid(): lax.conv_general_dilated(padded[None], kernel, (1, 1, 1), ((0, 0), (0, 0)...  86.7 us
    ppermute x4, waiting for transfers between devices, local_decode(): from_above = lax.ppermute(extended[:, row_count - 1:], 'hp', rows_down)  51.7 us
    broadcast_in_dim x4, local copies, waits for them, and re-layouts, conv_valid(): padded[None]  22.1 us
    ppermute x4, waiting for transfers between devices, local_decode(): prev_frames = lax.ppermute(activated[frames - 2:], 'cp', time_fwd)  20.2 us
    convert_element_type x4, other arithmetic, norm_silu(): jax.nn.silu(local_act.astype(jnp.float32) * scale_c + shift_c)  18.6 us
    ppermute x4, waiting for transfers between devices, local_decode(): from_below = lax.ppermute(extended[:, :1], 'hp', rows_up)  16.7 us
  transfers between devices with their start and end apart: 12, of which 12 were waited for; matrix products, arithmetic and copies ran while one was open for 0% of the time, Pallas kernels for 0%

commit v1 on v0

v1 whole, which is shorter than its diff:
```python
import functools

import jax
import jax.numpy as jnp
from jax import lax
from jax.experimental import pallas as pl
from jax.experimental.pallas import tpu as pltpu
from jax.sharding import PartitionSpec as P

GROUPS = 32
EPS = 1e-6
CHUNK = 4
MESH = pl.DeviceIdType.MESH
F32 = jnp.float32
BF16 = jnp.bfloat16


def group_sum(v, lane):
    n = v.shape[-1]
    v = v + jnp.where(lane % 2 == 0, pltpu.roll(v, n - 1, 1), pltpu.roll(v, 1, 1))
    return v + jnp.where(lane % 4 < 2, pltpu.roll(v, n - 2, 1), pltpu.roll(v, 2, 1))


def kernel(cfg, lat_ref, w_ref, bias_ref, gamma_ref, beta_ref, out_ref, raw_a, raw_b, act_a, act_b, w2_a, w2_b, stat,
           in_sem, out_sem, w_sem, row_send, row_recv, cp_send, cp_recv, st_send, st_recv):
    n_h, n_c, frames, rows, width, ch, total = cfg
    n_q = frames // CHUNK
    n_dev = n_h * n_c
    h = lax.axis_index("hp")
    c = lax.axis_index("cp")
    me = h * n_c + c
    has_up, has_down = h > 0, h < n_h - 1
    has_prev, has_next = c > 0, c < n_c - 1

    def device(idx):
        return {"hp": idx // n_c, "cp": lax.rem(idx, n_c)}

    barrier = pltpu.get_barrier_semaphore()
    for d in range(1, n_dev):
        pl.semaphore_signal(barrier, inc=1, device_id=device(lax.rem(me + d, n_dev)), device_id_type=MESH)

    def in_copy(k):
        return pltpu.make_async_copy(lat_ref.at[pl.ds(k * CHUNK, CHUNK)],
                                     raw_a.at[pl.ds(k * CHUNK + 2, CHUNK), 1:rows + 1], in_sem.at[k])

    for k in range(n_q):
        in_copy(k).start()

    def w_copies(layer, buf, which):
        return [pltpu.make_async_copy(w_ref.at[layer], buf.at[o:o + 3, :, :, :, o * ch:(o + 1) * ch], w_sem.at[which, o])
                for o in range(2)]

    for which, buf in enumerate((w2_a, w2_b)):
        for o in range(2):
            for i in range(3):
                for j in range(3):
                    buf[3 - 3 * o, i, j, :, o * ch:(o + 1) * ch] = jnp.zeros((ch, ch), BF16)
        for cp in w_copies(which, buf, which):
            cp.start()

    pl.semaphore_wait(barrier, n_dev - 1)

    raws = (raw_a, raw_b)

    def row_copy(k, buf, up, src=None):
        row = 0 if up else rows - 1
        fr = pl.ds(k * CHUNK + 2, CHUNK)
        source = raws[buf].at[fr, row + 1] if src is None else src.at[pl.ds(k * CHUNK, CHUNK), row]
        d = 0 if up else 1
        return pltpu.make_async_remote_copy(
            src_ref=source, dst_ref=raws[buf].at[fr, rows + 1 if up else 0],
            send_sem=row_send.at[buf, d, k], recv_sem=row_recv.at[buf, d, k],
            device_id={"hp": h - 1 if up else h + 1}, device_id_type=MESH)

    def row_start(k, buf, src=None):
        @pl.when(has_up)
        def _():
            row_copy(k, buf, True, src).start()

        @pl.when(has_down)
        def _():
            row_copy(k, buf, False, src).start()

    def row_wait(k, buf):
        @pl.when(has_down)
        def _():
            row_copy(k, buf, True).wait_recv()
            row_copy(k, buf, False).wait_send()

        @pl.when(has_up)
        def _():
            row_copy(k, buf, False).wait_recv()
            row_copy(k, buf, True).wait_send()

    def cp_copy(buf, part, src=None):
        lo, hi, dst_lo, dst_hi, dh = ((0, rows, 1, rows + 1, 0), (0, 1, rows + 1, rows + 2, -1),
                                      (rows - 1, rows, 0, 1, 1))[part]
        source = raws[buf].at[frames:frames + 2, lo + 1:hi + 1] if src is None else src.at[frames - 2:frames, lo:hi]
        return pltpu.make_async_remote_copy(
            src_ref=source, dst_ref=raws[buf].at[0:2, dst_lo:dst_hi],
            send_sem=cp_send.at[buf, part], recv_sem=cp_recv.at[buf, part],
            device_id={"hp": h + dh, "cp": c + 1}, device_id_type=MESH)

    def cp_start(buf, src=None):
        for part, cond in enumerate((has_next, has_next & has_up, has_next & has_down)):
            @pl.when(cond)
            def _():
                cp_copy(buf, part, src).start()

    def cp_wait(buf):
        for part, cond in enumerate((has_prev, has_prev & has_down, has_prev & has_up)):
            @pl.when(cond)
            def _():
                cp_copy(buf, part).wait_recv()
        for part, cond in enumerate((has_next, has_next & has_up, has_next & has_down)):
            @pl.when(cond)
            def _():
                cp_copy(buf, part).wait_send()

    def stat_copy(layer, d):
        return pltpu.make_async_remote_copy(
            src_ref=stat.at[layer, me], dst_ref=stat.at[layer, me],
            send_sem=st_send.at[layer, d], recv_sem=st_recv.at[layer, me],
            device_id=device(lax.rem(me + d, n_dev)), device_id_type=MESH)

    def stat_start(layer, s1, s2):
        stat[layer, me, 0:1, :] = jnp.sum(s1, axis=0, keepdims=True)
        stat[layer, me, 1:2, :] = jnp.sum(s2, axis=0, keepdims=True)
        for d in range(1, n_dev):
            stat_copy(layer, d).start()

    def stat_finish(layer):
        for d in range(1, n_dev):
            src = lax.rem(me + d, n_dev)
            pltpu.make_async_remote_copy(
                src_ref=stat.at[layer, src], dst_ref=stat.at[layer, src],
                send_sem=st_send.at[layer, d], recv_sem=st_recv.at[layer, src],
                device_id=device(src), device_id_type=MESH).wait_recv()
            stat_copy(layer, d).wait_send()
        lane = lax.broadcasted_iota(jnp.int32, (8, ch), 1)
        sums = jnp.sum(stat[layer], axis=0)
        s1 = group_sum(jnp.broadcast_to(sums[0:1], (8, ch)), lane)
        s2 = group_sum(jnp.broadcast_to(sums[1:2], (8, ch)), lane)
        mean = s1 / total
        inv = lax.rsqrt(s2 / total - mean * mean + EPS)
        scale = gamma_ref[pl.ds(layer, 1)] * inv
        shift = beta_ref[pl.ds(layer, 1)] - mean * scale
        return (0.5 * scale)[0:1], (0.5 * shift)[0:1]

    last = n_q - 1
    row_start(last, 0, lat_ref)
    row_start(last - 1, 0, lat_ref)

    def stats_of(v, s1, s2):
        v8 = v.reshape(v.shape[0] // 8, 8, ch)
        return s1 + jnp.sum(v8, axis=0), s2 + jnp.sum(v8 * v8, axis=0)

    zero = jnp.zeros((8, ch), F32)

    def x_stats(k, carry):
        in_copy(k).wait()
        s1, s2 = carry
        for f in range(CHUNK):
            for r in range(rows):
                s1, s2 = stats_of(raw_a[k * CHUNK + 2 + f, r + 1].astype(F32), s1, s2)
        return s1, s2

    stat_start(0, *lax.fori_loop(0, n_q, x_stats, (zero, zero)))
    for k in range(last - 2, -1, -1):
        row_start(k, 0, lat_ref)
    cp_start(0, lat_ref)

    sub = lax.broadcasted_iota(jnp.int32, (width, ch), 0)

    def norm_row(raw, frame, r, act, slot, scale, shift):
        t = raw[frame, r].astype(F32) * scale + shift
        v = t + t * jnp.tanh(t)
        if r == 0:
            v = jnp.where(has_up, v, 0.0)
        if r == rows + 1:
            v = jnp.where(has_down, v, 0.0)
        act[slot, r, :, 0:ch] = jnp.where(sub == 0, 0.0, pltpu.roll(v, 1, 0)).astype(BF16)
        act[slot, r, :, ch:2 * ch] = v.astype(BF16)
        act[slot, r, :, 2 * ch:3 * ch] = jnp.where(sub == width - 1, 0.0, pltpu.roll(v, width - 1, 0)).astype(BF16)

    first_frame = jnp.where(has_prev, 0, 2)

    def step(q, block, sub_idx, scale, shift, carry):
        src, dst = raws[sub_idx], raws[1 - sub_idx]
        parity = sub_idx
        act, nxt = (act_a, act_b) if step.even else (act_b, act_a)
        w2 = (w2_a, w2_b)[sub_idx]
        layer = 2 * block + sub_idx
        lhs = []
        for p in range(2):
            lhs.append(jnp.concatenate(
                [act[2 * p + k, i:i + rows].reshape(rows * width, 3 * ch) for k in range(4) for i in range(3)], axis=1))
        wmat = w2[...].reshape(36 * ch, 2 * ch)
        acc = jnp.dot(jnp.concatenate(lhs, axis=0), wmat, preferred_element_type=F32)
        base = jnp.maximum(q * CHUNK - CHUNK, 0)
        for f in range(CHUNK):
            frame = base + f if f >= 2 else jnp.maximum(base + f, first_frame)
            for r in range(rows + 2):
                norm_row(src, frame, r, nxt, f, scale, shift)
        nxt[CHUNK:CHUNK + 2] = act[0:2]
        s1, s2 = carry
        bias = bias_ref[pl.ds(layer, 1)]
        for p in range(2):
            for i in range(rows):
                for o in range(2):
                    at = (p * rows + i) * width
                    y = (acc[at:at + width, o * ch:(o + 1) * ch] + bias).astype(BF16)
                    frame = q * CHUNK + 2 + 2 * p + o
                    if sub_idx == 1:
                        y = (dst[frame, i + 1].astype(F32) + y.astype(F32)).astype(BF16)
                    dst[frame, i + 1] = y
                    s1, s2 = stats_of(y.astype(F32), s1, s2)
        return s1, s2

    def conv_layer(block, sub_idx, scale, shift):
        src = raws[sub_idx]
        for which in range(2):
            w_copies(sub_idx, (w2_a, w2_b)[sub_idx], sub_idx)[which].wait()
        row_wait(last, sub_idx)
        row_wait(last - 1, sub_idx)
        for f in range(CHUNK + 2):
            for r in range(rows + 2):
                norm_row(src, frames - CHUNK + f, r, act_a, f, scale, shift)

        def after(q):
            if sub_idx == 0:
                row_start(q, 1)
            else:
                @pl.when(block == 0)
                def _():
                    row_start(q, 0)

                @pl.when(block == 1)
                def _():
                    out_copy(q).start()

        def pair(i, carry):
            q = last - 2 * i

            @pl.when(i < n_q // 2 - 1)
            def _():
                row_wait(q - 2, sub_idx)

            @pl.when(i == n_q // 2 - 1)
            def _():
                cp_wait(sub_idx)

            step.even = True
            carry = step(q, block, sub_idx, scale, shift, carry)
            after(q)

            @pl.when(i == 0)
            def _():
                if sub_idx == 0:
                    cp_start(1)
                else:
                    @pl.when(block == 0)
                    def _():
                        cp_start(0)

            @pl.when(i < n_q // 2 - 1)
            def _():
                row_wait(q - 3, sub_idx)

            step.even = False
            carry = step(q - 1, block, sub_idx, scale, shift, carry)
            after(q - 1)
            return carry

        return lax.fori_loop(0, n_q // 2, pair, (zero, zero))

    def out_copy(q):
        return pltpu.make_async_copy(raw_a.at[pl.ds(q * CHUNK + 2, CHUNK), 1:rows + 1],
                                     out_ref.at[pl.ds(q * CHUNK, CHUNK)], out_sem.at[q])

    def block_body(block, _):
        scale, shift = stat_finish(2 * block)
        sums = conv_layer(block, 0, scale, shift)
        stat_start(2 * block + 1, *sums)

        @pl.when(block == 0)
        def _():
            for cp in w_copies(2, w2_a, 0):
                cp.start()

        scale, shift = stat_finish(2 * block + 1)
        sums = conv_layer(block, 1, scale, shift)

        @pl.when(block == 0)
        def _():
            stat_start(2, *sums)
            for cp in w_copies(3, w2_b, 1):
                cp.start()

        return 0

    lax.fori_loop(0, 2, block_body, 0)
    for q in range(n_q):
        out_copy(q).wait()


def solution(mesh):
    n_h, n_c = mesh.shape["hp"], mesh.shape["cp"]

    def local_decode(lat, conv_w, conv_b, gamma, beta):
        frames, rows, width, ch = lat.shape
        total = float(frames * n_c * rows * n_h * width * (ch // GROUPS))
        n_q = frames // CHUNK
        cfg = (n_h, n_c, frames, rows, width, ch, total)
        vmem = pl.BlockSpec(memory_space=pltpu.VMEM)
        anym = pl.BlockSpec(memory_space=pl.ANY)
        dma = pltpu.SemaphoreType.DMA
        return pl.pallas_call(
            functools.partial(kernel, cfg),
            out_shape=jax.ShapeDtypeStruct(lat.shape, lat.dtype),
            in_specs=[anym, anym, vmem, vmem, vmem],
            out_specs=anym,
            scratch_shapes=[
                pltpu.VMEM((frames + 2, rows + 2, width, ch), BF16),
                pltpu.VMEM((frames + 2, rows + 2, width, ch), BF16),
                pltpu.VMEM((CHUNK + 2, rows + 2, width, 3 * ch), BF16),
                pltpu.VMEM((CHUNK + 2, rows + 2, width, 3 * ch), BF16),
                pltpu.VMEM((4, 3, 3, ch, 2 * ch), BF16),
                pltpu.VMEM((4, 3, 3, ch, 2 * ch), BF16),
                pltpu.VMEM((4, n_h * n_c, 2, ch), F32),
                dma((n_q,)), dma((n_q,)), dma((2, 2)),
                dma((2, 2, n_q)), dma((2, 2, n_q)), dma((2, 3)), dma((2, 3)),
                dma((4, n_h * n_c)), dma((4, n_h * n_c)),
            ],
            compiler_params=pltpu.CompilerParams(collective_id=0, has_side_effects=True, vmem_limit_bytes=60 * 1024 * 1024),
        )(lat, conv_w, conv_b, gamma, beta)

    spec = P(("dp", "cp"), "hp", None, None)
    return jax.shard_map(local_decode, mesh=mesh, in_specs=(spec, P(), P(), P(), P()), out_specs=spec, check_vma=False)
```

time: 515 us -> 183 us (0.36)
  the two profiles are of different devices: /device:TPU:4 before, /device:TPU:0 now
where the time goes in v1:
time: 183 us; the launch traced here: 182 us
  Pallas kernels  179 us (98%)
  local copies, waits for them, and re-layouts  3.9 us (2%)
    pallas_call x1, Pallas kernels, local_decode(): pl.pallas_call(functools.partial(kernel, cfg), out_shape=jax.ShapeDtypeSt...  179 us
    unnamed x1, local copies, waits for them, and re-layouts  3.9 us

profile of v1, /device:TPU:0, one launch (start us, length us, event | category | flops | bytes accessed | tf_op | source)
XLA Modules:
  0.0 182.5 jit_solution(11892144298412908171)
XLA Ops:
  0.0 178.5 %shard_map.55 = bf16[32,4,96,128]{3,2,1,0:T(8,128)(2,1)} custom-call(bf16[32,4,96,128]{3,2,1,0:T(8,128)(2,1)} %lat_ref.1, bf16[4,3,3,3,128,128]{5,4,3,2,1,0:T(8,128)(2,1)} %w_ref.1, f32[4,128]{1,0:T(4,128)} %bias_ref.1, f32[4,128]{1,0:T(4,128)} %gamma_ref.1, f32[4,128]{1,0:T(4,128)} %beta_ref.1), custom_call_target="tpu_custom_call" | custom-call | tf_op jit(solution)/shard_map/pallas_call | solution.py:318
  178.6 3.9 %copy.7 = bf16[32,4,96,128]{3,2,1,0:T(8,128)(2,1)} copy(bf16[32,4,96,128]{3,2,1,0:T(8,128)(2,1)} %shard_map.55) | data formatting | bytes 6291456

commit v2 on v1

--- a/solution.py
+++ b/solution.py
@@ -10,6 +10,7 @@
 GROUPS = 32
 EPS = 1e-6
 CHUNK = 4
+PARTS = 6
 MESH = pl.DeviceIdType.MESH
 F32 = jnp.float32
 BF16 = jnp.bfloat16
@@ -21,7 +22,7 @@
     return v + jnp.where(lane % 4 < 2, pltpu.roll(v, n - 2, 1), pltpu.roll(v, 2, 1))
 
 
-def kernel(cfg, lat_ref, w_ref, bias_ref, gamma_ref, beta_ref, out_ref, raw_a, raw_b, act_a, act_b, w2_a, w2_b, stat,
+def kernel(cfg, lat_ref, w_ref, bias_ref, gamma_ref, beta_ref, out_ref, raw_a, raw_b, act_a, act_b, w2_a, w2_b, acc_buf, stat,
            in_sem, out_sem, w_sem, row_send, row_recv, cp_send, cp_recv, st_send, st_recv):
     n_h, n_c, frames, rows, width, ch, total = cfg
     n_q = frames // CHUNK
@@ -185,60 +186,74 @@
 
     first_frame = jnp.where(has_prev, 0, 2)
 
-    def step(q, block, sub_idx, scale, shift, carry):
-        src, dst = raws[sub_idx], raws[1 - sub_idx]
-        parity = sub_idx
-        act, nxt = (act_a, act_b) if step.even else (act_b, act_a)
+    def step(q, block, sub_idx, par, scale, shift, carry):
+        src = raws[sub_idx]
+        act, nxt = (act_a, act_b) if par == 0 else (act_b, act_a)
         w2 = (w2_a, w2_b)[sub_idx]
-        layer = 2 * block + sub_idx
-        lhs = []
+        base = jnp.maximum(q * CHUNK - CHUNK, 0)
+        sums = [carry]
+
+        def norm_item(f, r):
+            frame = base + f if f >= 2 else jnp.maximum(base + f, first_frame)
+            norm_row(src, frame, r, nxt, f, scale, shift)
+
+        def tail_item(p, i):
+            sums[0] = epilogue(q + 1, block, sub_idx, 1 - par, p, i, sums[0])
+
+        norms = [functools.partial(norm_item, f, r) for f in range(CHUNK) for r in range(rows + 2)]
+        tails = [functools.partial(tail_item, p, i) for i in range(rows) for p in range(2)]
+        items = []
+        for n in range(len(tails)):
+            items += norms[3 * n:3 * n + 3] + [tails[n]]
+        acc, done = [None, None], 0
+        for kt in range(PARTS):
+            weights = weight_part(w2, kt)
+            for p in range(2):
+                part = jnp.dot(lhs_part(act, p, kt), weights, preferred_element_type=F32)
+                acc[p] = part if acc[p] is None else acc[p] + part
+            upto = (kt + 1) * len(items) // PARTS
+            for item in items[done:upto]:
+                item()
+            done = upto
         for p in range(2):
-            lhs.append(jnp.concatenate(
-                [act[2 * p + k, i:i + rows].reshape(rows * width, 3 * ch) for k in range(4) for i in range(3)], axis=1))
-        wmat = w2[...].reshape(36 * ch, 2 * ch)
-        acc = jnp.dot(jnp.concatenate(lhs, axis=0), wmat, preferred_element_type=F32)
-        base = jnp.maximum(q * CHUNK - CHUNK, 0)
-        for f in range(CHUNK):
-            frame = base + f if f >= 2 else jnp.maximum(base + f, first_frame)
-            for r in range(rows + 2):
-                norm_row(src, frame, r, nxt, f, scale, shift)
+            acc_buf[par, p] = acc[p]
         nxt[CHUNK:CHUNK + 2] = act[0:2]
-        s1, s2 = carry
-        bias = bias_ref[pl.ds(layer, 1)]
-        for p in range(2):
-            for i in range(rows):
-                for o in range(2):
-                    at = (p * rows + i) * width
-                    y = (acc[at:at + width, o * ch:(o + 1) * ch] + bias).astype(BF16)
-                    frame = q * CHUNK + 2 + 2 * p + o
-                    if sub_idx == 1:
-                        y = (dst[frame, i + 1].astype(F32) + y.astype(F32)).astype(BF16)
-                    dst[frame, i + 1] = y
-                    s1, s2 = stats_of(y.astype(F32), s1, s2)
-        return s1, s2
+        return sums[0]
+
+    def blocks(kt):
+        n = 36 // PARTS
+        return [divmod(b, 3) for b in range(kt * n, (kt + 1) * n)]
+
+    def weight_part(w2, kt):
+        return jnp.concatenate([w2[n // 3, n % 3, j] for n, j in blocks(kt)], axis=0)
+
+    def lhs_part(act, p, kt):
+        return jnp.concatenate([act[2 * p + n // 3, n % 3:n % 3 + rows, :, j * ch:(j + 1) * ch].reshape(rows * width, ch)
+                                for n, j in blocks(kt)], axis=1)
+
+    def epilogue(q, block, sub_idx, par, p, i, sums):
+        dst = raws[1 - sub_idx]
+        acc = acc_buf[par, p, i * width:(i + 1) * width]
+        bias = bias_ref[pl.ds(2 * block + sub_idx, 1)]
+        for o in range(2):
+            y = (acc[:, o * ch:(o + 1) * ch] + bias).astype(BF16)
+            frame = q * CHUNK + 2 + 2 * p + o
+            if sub_idx == 1:
+                y = (dst[frame, i + 1].astype(F32) + y.astype(F32)).astype(BF16)
+            dst[frame, i + 1] = y
+            sums = stats_of(y.astype(F32), *sums)
+        return sums
 
     def conv_layer(block, sub_idx, scale, shift):
         src = raws[sub_idx]
-        for which in range(2):
-            w_copies(sub_idx, (w2_a, w2_b)[sub_idx], sub_idx)[which].wait()
+        for cp in w_copies(sub_idx, (w2_a, w2_b)[sub_idx], sub_idx):
+            cp.wait()
         row_wait(last, sub_idx)
         row_wait(last - 1, sub_idx)
         for f in range(CHUNK + 2):
             for r in range(rows + 2):
                 norm_row(src, frames - CHUNK + f, r, act_a, f, scale, shift)
 
-        def after(q):
-            if sub_idx == 0:
-                row_start(q, 1)
-            else:
-                @pl.when(block == 0)
-                def _():
-                    row_start(q, 0)
-
-                @pl.when(block == 1)
-                def _():
-                    out_copy(q).start()
-
         def pair(i, carry):
             q = last - 2 * i
 
@@ -250,9 +265,19 @@
             def _():
                 cp_wait(sub_idx)
 
-            step.even = True
-            carry = step(q, block, sub_idx, scale, shift, carry)
-            after(q)
+            s1, s2 = step(q, block, sub_idx, 0, scale, shift, carry)
+            carry = jnp.where(i == 0, 0.0, s1), jnp.where(i == 0, 0.0, s2)
+
+            @pl.when(i > 0)
+            def _():
+                after(q + 1, block, sub_idx)
+
+            @pl.when(i < n_q // 2 - 1)
+            def _():
+                row_wait(q - 3, sub_idx)
+
+            carry = step(q - 1, block, sub_idx, 1, scale, shift, carry)
+            after(q, block, sub_idx)
 
             @pl.when(i == 0)
             def _():
@@ -263,16 +288,25 @@
                     def _():
                         cp_start(0)
 
-            @pl.when(i < n_q // 2 - 1)
-            def _():
-                row_wait(q - 3, sub_idx)
-
-            step.even = False
-            carry = step(q - 1, block, sub_idx, scale, shift, carry)
-            after(q - 1)
             return carry
 
-        return lax.fori_loop(0, n_q // 2, pair, (zero, zero))
+        sums = lax.fori_loop(0, n_q // 2, pair, (zero, zero))
+        for i in range(rows):
+            for p in range(2):
+                sums = epilogue(0, block, sub_idx, 1, p, i, sums)
+        return sums
+
+    def after(q, block, sub_idx):
+        if sub_idx == 0:
+            row_start(q, 1)
+        else:
+            @pl.when(block == 0)
+            def _():
+                row_start(q, 0)
+
+            @pl.when(block == 1)
+            def _():
+                out_copy(q).start()
 
     def out_copy(q):
         return pltpu.make_async_copy(raw_a.at[pl.ds(q * CHUNK + 2, CHUNK), 1:rows + 1],
@@ -282,6 +316,7 @@
         scale, shift = stat_finish(2 * block)
         sums = conv_layer(block, 0, scale, shift)
         stat_start(2 * block + 1, *sums)
+        after(0, block, 0)
 
         @pl.when(block == 0)
         def _():
@@ -297,6 +332,7 @@
             for cp in w_copies(3, w2_b, 1):
                 cp.start()
 
+        after(0, block, 1)
         return 0
 
     lax.fori_loop(0, 2, block_body, 0)
@@ -321,12 +357,13 @@
             in_specs=[anym, anym, vmem, vmem, vmem],
             out_specs=anym,
             scratch_shapes=[
-                pltpu.VMEM((frames + 2, rows + 2, width, ch), BF16),
-                pltpu.VMEM((frames + 2, rows + 2, width, ch), BF16),
+                pltpu.VMEM((frames + 2 + CHUNK, rows + 2, width, ch), BF16),
+                pltpu.VMEM((frames + 2 + CHUNK, rows + 2, width, ch), BF16),
                 pltpu.VMEM((CHUNK + 2, rows + 2, width, 3 * ch), BF16),
                 pltpu.VMEM((CHUNK + 2, rows + 2, width, 3 * ch), BF16),
                 pltpu.VMEM((4, 3, 3, ch, 2 * ch), BF16),
                 pltpu.VMEM((4, 3, 3, ch, 2 * ch), BF16),
+                pltpu.VMEM((2, 2, rows * width, 2 * ch), F32),
                 pltpu.VMEM((4, n_h * n_c, 2, ch), F32),
                 dma((n_q,)), dma((n_q,)), dma((2, 2)),
                 dma((2, 2, n_q)), dma((2, 2, n_q)), dma((2, 3)), dma((2, 3)),

time: 183 us -> 118 us (0.64)
  Pallas kernels: 179 us -> 114 us
    pallas_call x1, Pallas kernels: 179 us -> 114 us  [local_decode(): pl.pallas_call(functools.partial(kernel, cfg), out_shape=jax.ShapeDtypeSt...]
where the time goes in v2:
time: 118 us
  Pallas kernels  114 us (97%)
  local copies, waits for them, and re-layouts  3.9 us (3%)
    pallas_call x1, Pallas kernels, local_decode(): pl.pallas_call(functools.partial(kernel, cfg), out_shape=jax.ShapeDtypeSt...  114 us
    unnamed x1, local copies, waits for them, and re-layouts  3.9 us

profile of v2, /device:TPU:0, one launch (start us, length us, event | category | flops | bytes accessed | tf_op | source)
XLA Modules:
  0.0 117.5 jit_solution(11679039925618398012)
XLA Ops:
  0.0 113.6 %shard_map.55 = bf16[32,4,96,128]{3,2,1,0:T(8,128)(2,1)} custom-call(bf16[32,4,96,128]{3,2,1,0:T(8,128)(2,1)} %lat_ref.1, bf16[4,3,3,3,128,128]{5,4,3,2,1,0:T(8,128)(2,1)} %w_ref.1, f32[4,128]{1,0:T(4,128)} %bias_ref.1, f32[4,128]{1,0:T(4,128)} %gamma_ref.1, f32[4,128]{1,0:T(4,128)} %beta_ref.1), custom_call_target="tpu_custom_call" | custom-call | tf_op jit(solution)/shard_map/pallas_call | solution.py:354
  113.6 3.9 %copy.7 = bf16[32,4,96,128]{3,2,1,0:T(8,128)(2,1)} copy(bf16[32,4,96,128]{3,2,1,0:T(8,128)(2,1)} %shard_map.55) | data formatting | bytes 6291456

commit v3 on v2

v3 whole, which is shorter than its diff:
```python
import functools

import jax
import jax.numpy as jnp
from jax import lax
from jax.experimental import pallas as pl
from jax.experimental.pallas import tpu as pltpu
from jax.sharding import PartitionSpec as P

GROUPS = 32
EPS = 1e-6
CHUNK = 4
MESH = pl.DeviceIdType.MESH
F32 = jnp.float32
BF16 = jnp.bfloat16


def group_sum(v, lane):
    n = v.shape[-1]
    v = v + jnp.where(lane % 2 == 0, pltpu.roll(v, n - 1, 1), pltpu.roll(v, 1, 1))
    return v + jnp.where(lane % 4 < 2, pltpu.roll(v, n - 2, 1), pltpu.roll(v, 2, 1))


def kernel(cfg, lat_ref, w_ref, bias_ref, gamma_ref, beta_ref, out_ref, raw_a, raw_b, act_a, act_b, wa_a, wa_b, wb_a, wb_b, acc_t, acc_r, stat,
           in_sem, out_sem, w_sem, row_send, row_recv, cp_send, cp_recv, st_send, st_recv):
    n_h, n_c, frames, rows, width, ch, total = cfg
    n_q = frames // CHUNK
    n_dev = n_h * n_c
    h = lax.axis_index("hp")
    c = lax.axis_index("cp")
    me = h * n_c + c
    has_up, has_down = h > 0, h < n_h - 1
    has_prev, has_next = c > 0, c < n_c - 1

    def device(idx):
        return {"hp": idx // n_c, "cp": lax.rem(idx, n_c)}

    barrier = pltpu.get_barrier_semaphore()
    for d in range(1, n_dev):
        pl.semaphore_signal(barrier, inc=1, device_id=device(lax.rem(me + d, n_dev)), device_id_type=MESH)

    def in_copy(k):
        return pltpu.make_async_copy(lat_ref.at[pl.ds(k * CHUNK, CHUNK)],
                                     raw_a.at[pl.ds(k * CHUNK + 2, CHUNK), 1:rows + 1], in_sem.at[k])

    for k in range(n_q):
        in_copy(k).start()

    wts = ((wa_a, wb_a), (wa_b, wb_b))

    def w_copies(layer, which):
        wa, wb = wts[which]
        pairs = [(w_ref.at[layer, 1:3], wa.at[:, :, :, :, 0:ch]), (w_ref.at[layer, 0:2], wa.at[:, :, :, :, ch:2 * ch])]
        for o in range(2):
            for n in range(2):
                pairs.append((w_ref.at[layer, 2 * o], wb.at[o, n:n + 3, :, :, n * ch:(n + 1) * ch]))
        return [pltpu.make_async_copy(src, dst, w_sem.at[which, n]) for n, (src, dst) in enumerate(pairs)]

    for which in range(2):
        wb = wts[which][1]
        for o in range(2):
            for j in range(3):
                for n in range(2):
                    wb[o, 3 - 3 * n, j, :, n * ch:(n + 1) * ch] = jnp.zeros((ch, ch), BF16)
        for cp in w_copies(which, which):
            cp.start()

    raws = (raw_a, raw_b)

    def row_copy(k, buf, up):
        fr = {0: pl.ds(2, CHUNK - 2), n_q: pl.ds(frames, 2)}.get(k, pl.ds(k * CHUNK, CHUNK)) if isinstance(k, int) else pl.ds(k * CHUNK, CHUNK)
        d = 0 if up else 1
        return pltpu.make_async_remote_copy(
            src_ref=raws[buf].at[fr, 1 if up else rows], dst_ref=raws[buf].at[fr, rows + 1 if up else 0],
            send_sem=row_send.at[buf, d, k], recv_sem=row_recv.at[buf, d, k],
            device_id={"hp": h - 1 if up else h + 1}, device_id_type=MESH)

    def rows_start(chunks, buf):
        for up, cond in ((True, has_up), (False, has_down)):
            @pl.when(cond)
            def _():
                for k in chunks:
                    row_copy(k, buf, up).start()

    def rows_wait(chunks, buf):
        for up, cond in ((True, has_down), (False, has_up)):
            @pl.when(cond)
            def _():
                for k in chunks:
                    row_copy(k, buf, up).wait_recv()
                    row_copy(k, buf, not up).wait_send()

    def cp_copy(buf, part, src=None):
        lo, hi, dst_lo, dst_hi, dh = ((0, rows, 1, rows + 1, 0), (0, 1, rows + 1, rows + 2, -1),
                                      (rows - 1, rows, 0, 1, 1))[part]
        source = raws[buf].at[frames:frames + 2, lo + 1:hi + 1] if src is None else src.at[frames - 2:frames, lo:hi]
        return pltpu.make_async_remote_copy(
            src_ref=source, dst_ref=raws[buf].at[0:2, dst_lo:dst_hi],
            send_sem=cp_send.at[buf, part], recv_sem=cp_recv.at[buf, part],
            device_id={"hp": h + dh, "cp": c + 1}, device_id_type=MESH)

    def cp_start(buf, src=None):
        for part, cond in enumerate((has_next, has_next & has_up, has_next & has_down)):
            @pl.when(cond)
            def _():
                cp_copy(buf, part, src).start()

    def cp_wait(buf):
        for part, cond in enumerate((has_prev, has_prev & has_down, has_prev & has_up)):
            @pl.when(cond)
            def _():
                cp_copy(buf, part).wait_recv()
        for part, cond in enumerate((has_next, has_next & has_up, has_next & has_down)):
            @pl.when(cond)
            def _():
                cp_copy(buf, part).wait_send()

    def stat_copy(layer, d):
        return pltpu.make_async_remote_copy(
            src_ref=stat.at[layer, me], dst_ref=stat.at[layer, me],
            send_sem=st_send.at[layer, d], recv_sem=st_recv.at[layer, me],
            device_id=device(lax.rem(me + d, n_dev)), device_id_type=MESH)

    def stat_start(layer, s1, s2):
        stat[layer, me, 0:1, :] = jnp.sum(s1, axis=0, keepdims=True)
        stat[layer, me, 1:2, :] = jnp.sum(s2, axis=0, keepdims=True)
        for d in range(1, n_dev):
            stat_copy(layer, d).start()

    def stat_finish(layer):
        for d in range(1, n_dev):
            src = lax.rem(me + d, n_dev)
            pltpu.make_async_remote_copy(
                src_ref=stat.at[layer, src], dst_ref=stat.at[layer, src],
                send_sem=st_send.at[layer, d], recv_sem=st_recv.at[layer, src],
                device_id=device(src), device_id_type=MESH).wait_recv()
            stat_copy(layer, d).wait_send()
        lane = lax.broadcasted_iota(jnp.int32, (8, ch), 1)
        sums = jnp.sum(stat[layer], axis=0)
        s1 = group_sum(jnp.broadcast_to(sums[0:1], (8, ch)), lane)
        s2 = group_sum(jnp.broadcast_to(sums[1:2], (8, ch)), lane)
        mean = s1 / total
        inv = lax.rsqrt(s2 / total - mean * mean + EPS)
        scale = gamma_ref[pl.ds(layer, 1)] * inv
        shift = beta_ref[pl.ds(layer, 1)] - mean * scale
        return (0.5 * scale)[0:1], (0.5 * shift)[0:1]

    last = n_q - 1

    def stats_of(v, s1, s2):
        v8 = v.reshape(v.shape[0] // 8, 8, ch)
        return s1 + jnp.sum(v8, axis=0), s2 + jnp.sum(v8 * v8, axis=0)

    zero = jnp.zeros((8, ch), F32)

    def x_stats(k, carry):
        in_copy(k).wait()
        s1, s2 = carry
        for f in range(CHUNK):
            for r in range(rows):
                s1, s2 = stats_of(raw_a[k * CHUNK + 2 + f, r + 1].astype(F32), s1, s2)
        return s1, s2

    sums = lax.fori_loop(0, n_q, x_stats, (zero, zero))
    pl.semaphore_wait(barrier, n_dev - 1)
    stat_start(0, *sums)
    rows_start(range(n_q, -1, -1), 0)
    cp_start(0)

    sub = lax.broadcasted_iota(jnp.int32, (8, ch), 0)

    def norm_row(raw, frame, r, act, slot, scale, shift):
        t = raw[frame, r].astype(F32) * scale + shift
        v = t + t * jnp.tanh(t)
        if r == 0:
            v = jnp.where(has_up, v, 0.0)
        if r == rows + 1:
            v = jnp.where(has_down, v, 0.0)
        left, right = pltpu.roll(v, 1, 0), pltpu.roll(v, width - 1, 0)
        left = jnp.concatenate([jnp.where(sub == 0, 0.0, left[:8]), left[8:]], axis=0)
        right = jnp.concatenate([right[:-8], jnp.where(sub == 7, 0.0, right[-8:])], axis=0)
        act[slot, r, :, 0:ch] = left.astype(BF16)
        act[slot, r, :, ch:2 * ch] = v.astype(BF16)
        act[slot, r, :, 2 * ch:3 * ch] = right.astype(BF16)

    first_frame = jnp.where(has_prev, 0, 2)

    def step(q, block, sub_idx, par, scale, shift, carry):
        src = raws[sub_idx]
        act, nxt = (act_a, act_b) if par == 0 else (act_b, act_a)
        wa, wb = wts[sub_idx]
        base = jnp.maximum(q * CHUNK - CHUNK, 0)
        sums = [carry]

        def norm_item(f, r):
            frame = base + f if f >= 2 else jnp.maximum(base + f, first_frame)
            norm_row(src, frame, r, nxt, f, scale, shift)

        def tail_item(p, i):
            sums[0] = epilogue(q + 1, block, sub_idx, 1 - par, p, i, sums[0])

        norms = [functools.partial(norm_item, f, r) for f in range(CHUNK) for r in range(rows + 2)]
        tails = [functools.partial(tail_item, p, i) for i in range(rows) for p in range(2)]
        items = []
        for n in range(len(tails)):
            items += norms[3 * n:3 * n + 3] + [tails[n]]
        parts = [functools.partial(row_part, act, wb, n) for n in range(2)] + [functools.partial(time_part, act, wa, n) for n in range(3)]
        weight = [2, 2, 3, 3, 3]
        acc, done = {}, 0
        for n, part in enumerate(parts):
            for key, value in part():
                acc[key] = acc[key] + value if key in acc else value
            if n == 1:
                for p in range(2):
                    for o in range(2):
                        acc_r[par, p, o] = acc[p, o]
            upto = sum(weight[:n + 1]) * len(items) // sum(weight)
            for item in items[done:upto]:
                item()
            done = upto
        for p in range(2):
            acc_t[par, p] = acc[p]
        nxt[CHUNK:CHUNK + 2] = act[0:2]
        return sums[0]

    def row_part(act, wb, n):
        for o in range(2):
            taps = [divmod(t, 3) for t in range(6 * n, 6 * n + 6)]
            weights = jnp.concatenate([wb[o, i, j] for i, j in taps], axis=0)
            for p in range(2):
                lhs = jnp.concatenate([
                    jnp.concatenate([act[2 * p + 3 * o, r + i, :, j * ch:(j + 1) * ch] for i, j in taps], axis=1)
                    for r in range(0, rows, 2)], axis=0)
                yield (p, o), jnp.dot(lhs, weights, preferred_element_type=F32)

    def time_part(act, wa, n):
        taps = [(t // 9, t // 3 % 3, t % 3) for t in range(6 * n, 6 * n + 6)]
        weights = jnp.concatenate([wa[k, i, j] for k, i, j in taps], axis=0)
        for p in range(2):
            lhs = jnp.concatenate([act[2 * p + 1 + k, i:i + rows, :, j * ch:(j + 1) * ch].reshape(rows * width, ch)
                                   for k, i, j in taps], axis=1)
            yield p, jnp.dot(lhs, weights, preferred_element_type=F32)

    def epilogue(q, block, sub_idx, par, p, i, sums):
        dst = raws[1 - sub_idx]
        acc = acc_t[par, p, i * width:(i + 1) * width]
        bias = bias_ref[pl.ds(2 * block + sub_idx, 1)]
        for o in range(2):
            two = acc_r[par, p, o, i // 2 * width:(i // 2 + 1) * width, i % 2 * ch:(i % 2 + 1) * ch]
            y = (acc[:, o * ch:(o + 1) * ch] + two + bias).astype(BF16)
            frame = q * CHUNK + 2 + 2 * p + o
            if sub_idx == 1:
                y = (dst[frame, i + 1].astype(F32) + y.astype(F32)).astype(BF16)
            dst[frame, i + 1] = y
            sums = stats_of(y.astype(F32), *sums)
        return sums

    def conv_layer(block, sub_idx, scale, shift):
        src = raws[sub_idx]
        for cp in w_copies(sub_idx, sub_idx):
            cp.wait()
        rows_wait((n_q, last), sub_idx)
        for f in range(CHUNK + 2):
            for r in range(rows + 2):
                norm_row(src, frames - CHUNK + f, r, act_a, f, scale, shift)

        def pair(i, carry):
            q = last - 2 * i

            @pl.when(i < n_q // 2 - 1)
            def _():
                rows_wait((q - 1, q - 2), sub_idx)

            @pl.when(i == n_q // 2 - 1)
            def _():
                rows_wait((0,), sub_idx)
                cp_wait(sub_idx)

            send(i, q, block, sub_idx)
            s1, s2 = step(q, block, sub_idx, 0, scale, shift, carry)
            carry = jnp.where(i == 0, 0.0, s1), jnp.where(i == 0, 0.0, s2)
            return step(q - 1, block, sub_idx, 1, scale, shift, carry)

        sums = lax.fori_loop(0, n_q // 2, pair, (zero, zero))
        for i in range(rows):
            for p in range(2):
                sums = epilogue(0, block, sub_idx, 1, p, i, sums)
        return sums

    def send(i, q, block, sub_idx):
        buf = 1 - sub_idx
        more = True if sub_idx == 0 else block == 0

        @pl.when((i == 1) & more)
        def _():
            rows_start((n_q,), buf)
            cp_start(buf)

        @pl.when((i > 1) & more)
        def _():
            rows_start((q + 4, q + 3), buf)

        if sub_idx == 1:
            @pl.when((i == 1) & (block == 1))
            def _():
                out_copy(last).start()

            @pl.when((i > 1) & (block == 1))
            def _():
                out_copy(q + 3).start()
                out_copy(q + 2).start()

    def send_rest(block, sub_idx):
        if sub_idx == 0:
            rows_start((3, 2, 1, 0), 1)
        else:
            @pl.when(block == 0)
            def _():
                rows_start((3, 2, 1, 0), 0)

            @pl.when(block == 1)
            def _():
                for q in (2, 1, 0):
                    out_copy(q).start()

    def out_copy(q):
        return pltpu.make_async_copy(raw_a.at[pl.ds(q * CHUNK + 2, CHUNK), 1:rows + 1],
                                     out_ref.at[pl.ds(q * CHUNK, CHUNK)], out_sem.at[q])

    def block_body(block, _):
        scale, shift = stat_finish(2 * block)
        sums = conv_layer(block, 0, scale, shift)
        stat_start(2 * block + 1, *sums)
        send_rest(block, 0)

        @pl.when(block == 0)
        def _():
            for cp in w_copies(2, 0):
                cp.start()

        scale, shift = stat_finish(2 * block + 1)
        sums = conv_layer(block, 1, scale, shift)

        @pl.when(block == 0)
        def _():
            stat_start(2, *sums)
            for cp in w_copies(3, 1):
                cp.start()

        send_rest(block, 1)
        return 0

    lax.fori_loop(0, 2, block_body, 0)
    for q in range(n_q):
        out_copy(q).wait()


def solution(mesh):
    n_h, n_c = mesh.shape["hp"], mesh.shape["cp"]

    def local_decode(lat, conv_w, conv_b, gamma, beta):
        frames, rows, width, ch = lat.shape
        total = float(frames * n_c * rows * n_h * width * (ch // GROUPS))
        n_q = frames // CHUNK
        cfg = (n_h, n_c, frames, rows, width, ch, total)
        vmem = pl.BlockSpec(memory_space=pltpu.VMEM)
        hbm = pl.BlockSpec(memory_space=pltpu.HBM)
        dma = pltpu.SemaphoreType.DMA
        return pl.pallas_call(
            functools.partial(kernel, cfg),
            out_shape=jax.ShapeDtypeStruct(lat.shape, lat.dtype),
            in_specs=[hbm, hbm, vmem, vmem, vmem],
            out_specs=pl.BlockSpec(memory_space=pl.ANY),
            scratch_shapes=[
                pltpu.VMEM((frames + 2 + CHUNK, rows + 2, width, ch), BF16),
                pltpu.VMEM((frames + 2 + CHUNK, rows + 2, width, ch), BF16),
                pltpu.VMEM((CHUNK + 2, rows + 2, width, 3 * ch), BF16),
                pltpu.VMEM((CHUNK + 2, rows + 2, width, 3 * ch), BF16),
                pltpu.VMEM((2, 3, 3, ch, 2 * ch), BF16),
                pltpu.VMEM((2, 3, 3, ch, 2 * ch), BF16),
                pltpu.VMEM((2, 4, 3, ch, 2 * ch), BF16),
                pltpu.VMEM((2, 4, 3, ch, 2 * ch), BF16),
                pltpu.VMEM((2, 2, rows * width, 2 * ch), F32),
                pltpu.VMEM((2, 2, 2, rows // 2 * width, 2 * ch), F32),
                pltpu.VMEM((4, n_h * n_c, 2, ch), F32),
                dma((n_q,)), dma((n_q,)), dma((2, 6)),
                dma((2, 2, n_q + 1)), dma((2, 2, n_q + 1)), dma((2, 3)), dma((2, 3)),
                dma((4, n_h * n_c)), dma((4, n_h * n_c)),
            ],
            compiler_params=pltpu.CompilerParams(collective_id=0, has_side_effects=True, vmem_limit_bytes=46 * 1024 * 1024),
        )(lat, conv_w, conv_b, gamma, beta)

    spec = P(("dp", "cp"), "hp", None, None)
    return jax.shard_map(local_decode, mesh=mesh, in_specs=(spec, P(), P(), P(), P()), out_specs=spec, check_vma=False)
```

time: 118 us -> 103 us (0.87)
  Pallas kernels: 114 us -> 97 us
  local copies, waits for them, and re-layouts: 3.9 us -> 5.6 us
    pallas_call x1, Pallas kernels: 114 us -> 97 us  [local_decode(): pl.pallas_call(functools.partial(kernel, cfg), out_shape=jax.ShapeDtypeSt...]
    unnamed x1 -> x9, local copies, waits for them, and re-layouts: 3.9 us -> 5.6 us
where the time goes in v3:
time: 103 us
  Pallas kernels  97 us (94%)
  local copies, waits for them, and re-layouts  5.6 us (5%)
    pallas_call x1, Pallas kernels, local_decode(): pl.pallas_call(functools.partial(kernel, cfg), out_shape=jax.ShapeDtypeSt...  97 us
    unnamed x9, local copies, waits for them, and re-layouts  5.6 us

profile of v3, /device:TPU:0, one launch (start us, length us, event | category | flops | bytes accessed | tf_op | source)
XLA Modules:
  0.0 102.6 jit_solution(13141719736697486873)
XLA Ops:
  0.0 0.0 copy-start
  0.0 1.9 %copy-done = bf16[32,4,96,128]{3,2,1,0:T(8,128)(2,1)S(1)} copy-done((bf16[32,4,96,128]{3,2,1,0:T(8,128)(2,1)S(1)}, bf16[32,4,96,128]{3,2,1,0:T(8,128)(2,1)}, u32[]{:S(2)}) %copy-start) | copy-done | bytes 3145752
  1.9 0.0 copy-start.1
  1.9 0.7 copy-done.1
  2.6 0.0 copy-start.2
  2.6 0.7 copy-done.2
  3.3 0.0 copy-start.3
  3.3 0.7 copy-done.3
  3.9 97.0 %shard_map.55 = bf16[32,4,96,128]{3,2,1,0:T(8,128)(2,1)S(1)} custom-call(bf16[32,4,96,128]{3,2,1,0:T(8,128)(2,1)S(1)} %copy-done, bf16[4,3,3,3,128,128]{5,4,3,2,1,0:T(8,128)(2,1)} %w_ref.1, f32[4,128]{1,0:T(4,128)S(1)} %copy-done.1, f32[4,128]{1,0:T(4,128)S(1)} %copy-done.2, f32[4,128]{1,0:T(4,128)S(1)} %copy-done.3), custom_call_target="tpu_custom_call" | custom-call | tf_op jit(solution)/shard_map/pallas_call | solution.py:369
  100.9 1.7 %copy.7 = bf16[32,4,96,128]{3,2,1,0:T(8,128)(2,1)} copy(bf16[32,4,96,128]{3,2,1,0:T(8,128)(2,1)S(1)} %shard_map.55) | data formatting | bytes 6291456
Async XLA Ops:
  0.0 1.9 %copy-start = (bf16[32,4,96,128]{3,2,1,0:T(8,128)(2,1)S(1)}, bf16[32,4,96,128]{3,2,1,0:T(8,128)(2,1)}, u32[]{:S(2)}) copy-start(bf16[32,4,96,128]{3,2,1,0:T(8,128)(2,1)} %lat_ref.1) | copy-start | bytes 9437188
  1.9 0.7 copy-start.1
  2.6 0.7 copy-start.2
  3.3 0.7 copy-start.3

commit v4 on v3

--- a/solution.py
+++ b/solution.py
@@ -22,7 +22,7 @@
 
 
 def kernel(cfg, lat_ref, w_ref, bias_ref, gamma_ref, beta_ref, out_ref, raw_a, raw_b, act_a, act_b, wa_a, wa_b, wb_a, wb_b, acc_t, acc_r, stat,
-           in_sem, out_sem, w_sem, row_send, row_recv, cp_send, cp_recv, st_send, st_recv):
+           in_sem, w_sem, row_send, row_recv, cp_send, cp_recv, st_send, st_recv):
     n_h, n_c, frames, rows, width, ch, total = cfg
     n_q = frames // CHUNK
     n_dev = n_h * n_c
@@ -50,10 +50,10 @@
 
     def w_copies(layer, which):
         wa, wb = wts[which]
-        pairs = [(w_ref.at[layer, 1:3], wa.at[:, :, :, :, 0:ch]), (w_ref.at[layer, 0:2], wa.at[:, :, :, :, ch:2 * ch])]
+        pairs = [(w_ref.at[layer, 1:3], wa.at[0]), (w_ref.at[layer, 0:2], wa.at[1])]
         for o in range(2):
             for n in range(2):
-                pairs.append((w_ref.at[layer, 2 * o], wb.at[o, n:n + 3, :, :, n * ch:(n + 1) * ch]))
+                pairs.append((w_ref.at[layer, 2 * o], wb.at[n, o, n:n + 3]))
         return [pltpu.make_async_copy(src, dst, w_sem.at[which, n]) for n, (src, dst) in enumerate(pairs)]
 
     for which in range(2):
@@ -61,10 +61,7 @@
         for o in range(2):
             for j in range(3):
                 for n in range(2):
-                    wb[o, 3 - 3 * n, j, :, n * ch:(n + 1) * ch] = jnp.zeros((ch, ch), BF16)
-        for cp in w_copies(which, which):
-            cp.start()
-
+                    wb[n, o, 3 - 3 * n, j] = jnp.zeros((ch, ch), BF16)
     raws = (raw_a, raw_b)
 
     def row_copy(k, buf, up):
@@ -75,9 +72,9 @@
             send_sem=row_send.at[buf, d, k], recv_sem=row_recv.at[buf, d, k],
             device_id={"hp": h - 1 if up else h + 1}, device_id_type=MESH)
 
-    def rows_start(chunks, buf):
+    def rows_start(chunks, buf, gate=True):
         for up, cond in ((True, has_up), (False, has_down)):
-            @pl.when(cond)
+            @pl.when(cond & gate)
             def _():
                 for k in chunks:
                     row_copy(k, buf, up).start()
@@ -134,7 +131,6 @@
                 src_ref=stat.at[layer, src], dst_ref=stat.at[layer, src],
                 send_sem=st_send.at[layer, d], recv_sem=st_recv.at[layer, src],
                 device_id=device(src), device_id_type=MESH).wait_recv()
-            stat_copy(layer, d).wait_send()
         lane = lax.broadcasted_iota(jnp.int32, (8, ch), 1)
         sums = jnp.sum(stat[layer], axis=0)
         s1 = group_sum(jnp.broadcast_to(sums[0:1], (8, ch)), lane)
@@ -162,6 +158,9 @@
         return s1, s2
 
     sums = lax.fori_loop(0, n_q, x_stats, (zero, zero))
+    for which in range(2):
+        for cp in w_copies(which, which):
+            cp.start()
     pl.semaphore_wait(barrier, n_dev - 1)
     stat_start(0, *sums)
     rows_start(range(n_q, -1, -1), 0)
@@ -179,13 +178,13 @@
         left, right = pltpu.roll(v, 1, 0), pltpu.roll(v, width - 1, 0)
         left = jnp.concatenate([jnp.where(sub == 0, 0.0, left[:8]), left[8:]], axis=0)
         right = jnp.concatenate([right[:-8], jnp.where(sub == 7, 0.0, right[-8:])], axis=0)
-        act[slot, r, :, 0:ch] = left.astype(BF16)
-        act[slot, r, :, ch:2 * ch] = v.astype(BF16)
-        act[slot, r, :, 2 * ch:3 * ch] = right.astype(BF16)
+        act[slot, r, 0] = left.astype(BF16)
+        act[slot, r, 1] = v.astype(BF16)
+        act[slot, r, 2] = right.astype(BF16)
 
     first_frame = jnp.where(has_prev, 0, 2)
 
-    def step(q, block, sub_idx, par, scale, shift, carry):
+    def step(q, block, sub_idx, par, scale, shift, carry, first=False):
         src = raws[sub_idx]
         act, nxt = (act_a, act_b) if par == 0 else (act_b, act_a)
         wa, wb = wts[sub_idx]
@@ -201,43 +200,49 @@
 
         norms = [functools.partial(norm_item, f, r) for f in range(CHUNK) for r in range(rows + 2)]
         tails = [functools.partial(tail_item, p, i) for i in range(rows) for p in range(2)]
-        items = []
-        for n in range(len(tails)):
-            items += norms[3 * n:3 * n + 3] + [tails[n]]
-        parts = [functools.partial(row_part, act, wb, n) for n in range(2)] + [functools.partial(time_part, act, wa, n) for n in range(3)]
-        weight = [2, 2, 3, 3, 3]
-        acc, done = {}, 0
+        parts = ([functools.partial(row_part, act, wb, o, n) for o in range(2) for n in range(2)]
+                 + [functools.partial(time_part, act, wa, n) for n in range(3)])
+        if first:
+            def own(f):
+                return [functools.partial(norm_row, src, frames - CHUNK + f, r, act, f, scale, shift) for r in range(rows + 2)]
+
+            for item in own(0) + own(2):
+                item()
+            beside = [own(3), own(5), own(1), own(4), norms[:8], norms[8:16], norms[16:]]
+        else:
+            items = []
+            for n in range(len(tails)):
+                items += norms[3 * n:3 * n + 3] + [tails[n]]
+            edges = [len(items) * n // 10 for n in (0, 1, 2, 3, 4, 6, 8, 10)]
+            beside = [items[lo:hi] for lo, hi in zip(edges, edges[1:])]
+        acc = {}
         for n, part in enumerate(parts):
             for key, value in part():
                 acc[key] = acc[key] + value if key in acc else value
-            if n == 1:
+            if n in (1, 3):
                 for p in range(2):
-                    for o in range(2):
-                        acc_r[par, p, o] = acc[p, o]
-            upto = sum(weight[:n + 1]) * len(items) // sum(weight)
-            for item in items[done:upto]:
+                    acc_r[par, p, n // 2] = acc[p, n // 2]
+            for item in beside[n]:
                 item()
-            done = upto
         for p in range(2):
             acc_t[par, p] = acc[p]
         nxt[CHUNK:CHUNK + 2] = act[0:2]
         return sums[0]
 
-    def row_part(act, wb, n):
-        for o in range(2):
-            taps = [divmod(t, 3) for t in range(6 * n, 6 * n + 6)]
-            weights = jnp.concatenate([wb[o, i, j] for i, j in taps], axis=0)
-            for p in range(2):
-                lhs = jnp.concatenate([
-                    jnp.concatenate([act[2 * p + 3 * o, r + i, :, j * ch:(j + 1) * ch] for i, j in taps], axis=1)
-                    for r in range(0, rows, 2)], axis=0)
-                yield (p, o), jnp.dot(lhs, weights, preferred_element_type=F32)
+    def row_part(act, wb, o, n):
+        taps = [divmod(t, 3) for t in range(6 * n, 6 * n + 6)]
+        weights = jnp.concatenate([jnp.concatenate([wb[n2, o, i, j] for i, j in taps], axis=0) for n2 in range(2)], axis=1)
+        for p in range(2):
+            lhs = jnp.concatenate([
+                jnp.concatenate([act[2 * p + 3 * o, r + i, j] for i, j in taps], axis=1)
+                for r in range(0, rows, 2)], axis=0)
+            yield (p, o), jnp.dot(lhs, weights, preferred_element_type=F32)
 
     def time_part(act, wa, n):
         taps = [(t // 9, t // 3 % 3, t % 3) for t in range(6 * n, 6 * n + 6)]
-        weights = jnp.concatenate([wa[k, i, j] for k, i, j in taps], axis=0)
+        weights = jnp.concatenate([jnp.concatenate([wa[n2, k, i, j] for k, i, j in taps], axis=0) for n2 in range(2)], axis=1)
         for p in range(2):
-            lhs = jnp.concatenate([act[2 * p + 1 + k, i:i + rows, :, j * ch:(j + 1) * ch].reshape(rows * width, ch)
+            lhs = jnp.concatenate([act[2 * p + 1 + k, i:i + rows, j].reshape(rows * width, ch)
                                    for k, i, j in taps], axis=1)
             yield p, jnp.dot(lhs, weights, preferred_element_type=F32)
 
@@ -252,6 +257,8 @@
             if sub_idx == 1:
                 y = (dst[frame, i + 1].astype(F32) + y.astype(F32)).astype(BF16)
             dst[frame, i + 1] = y
+            if sub_idx == 1:
+                out_ref[frame - 2, i] = y
             sums = stats_of(y.astype(F32), *sums)
         return sums
 
@@ -259,10 +266,9 @@
         src = raws[sub_idx]
         for cp in w_copies(sub_idx, sub_idx):
             cp.wait()
-        rows_wait((n_q, last), sub_idx)
-        for f in range(CHUNK + 2):
-            for r in range(rows + 2):
-                norm_row(src, frames - CHUNK + f, r, act_a, f, scale, shift)
+        rows_wait((n_q, last, last - 1, last - 2), sub_idx)
+        carry = step(last, block, sub_idx, 0, scale, shift, (zero, zero), first=True)
+        carry = step(last - 1, block, sub_idx, 1, scale, shift, carry)
 
         def pair(i, carry):
             q = last - 2 * i
@@ -277,11 +283,10 @@
                 cp_wait(sub_idx)
 
             send(i, q, block, sub_idx)
-            s1, s2 = step(q, block, sub_idx, 0, scale, shift, carry)
-            carry = jnp.where(i == 0, 0.0, s1), jnp.where(i == 0, 0.0, s2)
+            carry = step(q, block, sub_idx, 0, scale, shift, carry)
             return step(q - 1, block, sub_idx, 1, scale, shift, carry)
 
-        sums = lax.fori_loop(0, n_q // 2, pair, (zero, zero))
+        sums = lax.fori_loop(1, n_q // 2, pair, carry)
         for i in range(rows):
             for p in range(2):
                 sums = epilogue(0, block, sub_idx, 1, p, i, sums)
@@ -296,36 +301,16 @@
             rows_start((n_q,), buf)
             cp_start(buf)
 
-        @pl.when((i > 1) & more)
-        def _():
-            rows_start((q + 4, q + 3), buf)
-
-        if sub_idx == 1:
-            @pl.when((i == 1) & (block == 1))
-            def _():
-                out_copy(last).start()
-
-            @pl.when((i > 1) & (block == 1))
-            def _():
-                out_copy(q + 3).start()
-                out_copy(q + 2).start()
+        rows_start((7, 6), buf, (i == 2) & more)
+        rows_start((5,), buf, (i == 3) & more)
 
     def send_rest(block, sub_idx):
         if sub_idx == 0:
-            rows_start((3, 2, 1, 0), 1)
+            rows_start((4, 3, 2, 1, 0), 1)
         else:
             @pl.when(block == 0)
             def _():
-                rows_start((3, 2, 1, 0), 0)
-
-            @pl.when(block == 1)
-            def _():
-                for q in (2, 1, 0):
-                    out_copy(q).start()
-
-    def out_copy(q):
-        return pltpu.make_async_copy(raw_a.at[pl.ds(q * CHUNK + 2, CHUNK), 1:rows + 1],
-                                     out_ref.at[pl.ds(q * CHUNK, CHUNK)], out_sem.at[q])
+                rows_start((4, 3, 2, 1, 0), 0)
 
     def block_body(block, _):
         scale, shift = stat_finish(2 * block)
@@ -351,8 +336,9 @@
         return 0
 
     lax.fori_loop(0, 2, block_body, 0)
-    for q in range(n_q):
-        out_copy(q).wait()
+    for layer in range(4):
+        for d in range(1, n_dev):
+            stat_copy(layer, d).wait_send()
 
 
 def solution(mesh):
@@ -370,24 +356,24 @@
             functools.partial(kernel, cfg),
             out_shape=jax.ShapeDtypeStruct(lat.shape, lat.dtype),
             in_specs=[hbm, hbm, vmem, vmem, vmem],
-            out_specs=pl.BlockSpec(memory_space=pl.ANY),
+            out_specs=vmem,
             scratch_shapes=[
                 pltpu.VMEM((frames + 2 + CHUNK, rows + 2, width, ch), BF16),
                 pltpu.VMEM((frames + 2 + CHUNK, rows + 2, width, ch), BF16),
-                pltpu.VMEM((CHUNK + 2, rows + 2, width, 3 * ch), BF16),
-                pltpu.VMEM((CHUNK + 2, rows + 2, width, 3 * ch), BF16),
-                pltpu.VMEM((2, 3, 3, ch, 2 * ch), BF16),
-                pltpu.VMEM((2, 3, 3, ch, 2 * ch), BF16),
-                pltpu.VMEM((2, 4, 3, ch, 2 * ch), BF16),
-                pltpu.VMEM((2, 4, 3, ch, 2 * ch), BF16),
+                pltpu.VMEM((CHUNK + 2, rows + 2, 3, width, ch), BF16),
+                pltpu.VMEM((CHUNK + 2, rows + 2, 3, width, ch), BF16),
+                pltpu.VMEM((2, 2, 3, 3, ch, ch), BF16),
+                pltpu.VMEM((2, 2, 3, 3, ch, ch), BF16),
+                pltpu.VMEM((2, 2, 4, 3, ch, ch), BF16),
+                pltpu.VMEM((2, 2, 4, 3, ch, ch), BF16),
                 pltpu.VMEM((2, 2, rows * width, 2 * ch), F32),
                 pltpu.VMEM((2, 2, 2, rows // 2 * width, 2 * ch), F32),
                 pltpu.VMEM((4, n_h * n_c, 2, ch), F32),
-                dma((n_q,)), dma((n_q,)), dma((2, 6)),
+                dma((n_q,)), dma((2, 6)),
                 dma((2, 2, n_q + 1)), dma((2, 2, n_q + 1)), dma((2, 3)), dma((2, 3)),
                 dma((4, n_h * n_c)), dma((4, n_h * n_c)),
             ],
-            compiler_params=pltpu.CompilerParams(collective_id=0, has_side_effects=True, vmem_limit_bytes=46 * 1024 * 1024),
+            compiler_params=pltpu.CompilerParams(collective_id=0, has_side_effects=True, vmem_limit_bytes=50 * 1024 * 1024),
         )(lat, conv_w, conv_b, gamma, beta)
 
     spec = P(("dp", "cp"), "hp", None, None)

time: 103 us -> 95.5 us (0.927)
  Pallas kernels: 97 us -> 91.6 us
  local copies, waits for them, and re-layouts: 5.6 us -> 3.71 us
    pallas_call x1, Pallas kernels: 97 us -> 91.6 us  [local_decode(): pl.pallas_call(functools.partial(kernel, cfg), out_shape=jax.ShapeDtypeSt...]
    unnamed x9 -> x7, local copies, waits for them, and re-layouts: 5.6 us -> 3.71 us
where the time goes in v4:
time: 95.5 us; the launch traced here: 95.4 us
  Pallas kernels  91.6 us (96%)
  local copies, waits for them, and re-layouts  3.71 us (4%)
    pallas_call x1, Pallas kernels, local_decode(): pl.pallas_call(functools.partial(kernel, cfg), out_shape=jax.ShapeDtypeSt...  91.6 us
    unnamed x7, local copies, waits for them, and re-layouts  3.71 us

profile of v4, /device:TPU:0, one launch (start us, length us, event | category | flops | bytes accessed | tf_op | source)
XLA Modules:
  0.0 95.4 jit_solution(1397757453273104268)
XLA Ops:
  0.0 0.0 copy-start
  0.0 0.7 copy-done
  0.7 0.0 copy-start.1
  0.7 0.7 copy-done.1
  1.4 0.0 copy-start.2
  1.4 0.7 copy-done.2
  2.0 91.6 %shard_map.55 = bf16[32,4,96,128]{3,2,1,0:T(8,128)(2,1)S(1)} custom-call(bf16[32,4,96,128]{3,2,1,0:T(8,128)(2,1)} %lat_ref.1, bf16[4,3,3,3,128,128]{5,4,3,2,1,0:T(8,128)(2,1)} %w_ref.1, f32[4,128]{1,0:T(4,128)S(1)} %copy-done, f32[4,128]{1,0:T(4,128)S(1)} %copy-done.1, f32[4,128]{1,0:T(4,128)S(1)} %copy-done.2), custom_call_target="tpu_custom_call" | custom-call | tf_op jit(solution)/shard_map/pallas_call | solution.py:355
  93.7 1.7 %copy.7 = bf16[32,4,96,128]{3,2,1,0:T(8,128)(2,1)} copy(bf16[32,4,96,128]{3,2,1,0:T(8,128)(2,1)S(1)} %shard_map.55) | data formatting | bytes 6291456
Async XLA Ops:
  0.0 0.7 copy-start
  0.7 0.7 copy-start.1
  1.4 0.7 copy-start.2
